TPU v7x, 32 devices: a whole 2x2x4 slice. The times are simulated.
32 devices in a mesh: cells: 8 (over y, x, core), wells: 4 (over z).
Axes of the slice: x: 2, y: 2, z: 4, core: 2. Of those that a mesh axis runs over, the one named last changes fastest.
Arguments:
- cell_state: float32 [3, 4, 131072], P(None, 'wells', 'cells'), may hold values from -6 to 6
- cell_residual: float32 [3, 4, 131072], P(None, 'wells', 'cells'), may hold values from -6 to 6
- cell_block: float32 [9, 4, 131072], P(None, 'wells', 'cells'), may hold values from -4 to 4
- block_inverse: float32 [9, 4, 131072], P(None, 'wells', 'cells'), may hold values from -3.5 to 3.5
- perf_cells: int32 [4, 32, 128], P('wells'), may hold values from 0 to 131071, as said below
- perf_count: int32 [4, 32], P('wells'), may hold values from 32 to 128
- perf_index: float32 [4, 32, 128], P('wells'), may hold values from 0.2 to 2
- seg_parent: int32 [4, 32, 32], P('wells'), may hold values from 0 to 30, as said below
- seg_cond: float32 [4, 32, 32], P('wells'), may hold values from 0.5 to 4
- seg_state: float32 [3, 4, 32, 32], P(None, 'wells'), may hold values from -6 to 6
- seg_source: float32 [3, 4, 32, 32], P(None, 'wells'), may hold values from -6 to 6
Outputs:
- cell_update: float32 [3, 4, 131072], P(None, 'wells', 'cells')
- well_update: float32 [3, 4, 32, 32], P(None, 'wells', 'cells')
- residual_max: float32 [6], replicated
Inputs may be any that keep to these rules, and one draw needn't show every extreme that they name: seg_parent[..., 0] is 0; for s >= 1, seg_parent[..., s] lies between s - 3 and s - 1, so the segments of a well form a tree rooted at segment 0. `perf_cells`: in each region, take the wells in groups of 4 consecutive wells and the cells in blocks of 16384 consecutive cells; exactly 64 slots of each group, live or not, name a cell of each block.
All inputs are finite; a program needn't handle non-finite values.
Results may differ from a plain program's by a relative error of at most 0.0001.
Values sent between devices are 32-bit elements; how exact they have to be, the bound alone decides.
A program may use at most 128 MiB of HBM per device.

v0:
```python
import jax
import jax.numpy as jnp
from jax import lax
from jax.sharding import PartitionSpec as P


def expand_segments(values, slots):
    repeat = slots // values.shape[-1]
    wide = jnp.broadcast_to(values[..., None], values.shape + (repeat,))
    return wide.reshape(values.shape[:-1] + (slots,))


def segment_sums(values, segs):
    return jnp.sum(values.reshape(values.shape[:-1] + (segs, values.shape[-1] // segs)), axis=-1)


def perf_terms(jac_at, state_at, weight, seg_values):
    slots = weight.shape[-1]
    blocks = jac_at.reshape((3, 3) + weight.shape)
    kmat = jnp.sum(blocks[:, None] * blocks[None, :], axis=2)
    kmat = (kmat + jnp.eye(3, dtype=jnp.float32)[:, :, None, None]) * weight[None, None]
    differ = state_at - expand_segments(seg_values, slots)
    flow = jnp.sum(kmat * differ[None], axis=1)
    return (kmat, flow)


def solve_wells(ksum, rsum, parent, cond):
    segs = parent.shape[-1]
    count = parent.shape[0]
    index = jnp.arange(segs, dtype=jnp.int32)
    link = (parent[:, :, None] == index[None, None, :]) & (index[None, :, None] >= 1)
    adjacent = jnp.where(link, cond[:, :, None], jnp.float32(0.0))
    symmetric = adjacent + jnp.swapaxes(adjacent, 1, 2)
    eye_seg = jnp.eye(segs, dtype=jnp.float32)
    matrix = jnp.sum(symmetric, axis=2)[:, :, None] * eye_seg[None] - symmetric + eye_seg[None]
    eye_comp = jnp.eye(3, dtype=jnp.float32)
    blocks = jnp.transpose(ksum, (2, 3, 0, 1))
    dense = (
        matrix[:, :, None, :, None] * eye_comp[None, None, :, None, :]
        + blocks[:, :, :, None, :] * eye_seg[None, :, None, :, None]
    )
    dense = dense.reshape(count, 3 * segs, 3 * segs)
    rhs = jnp.transpose(rsum, (1, 2, 0)).reshape(count, 3 * segs)
    lower = jnp.linalg.cholesky(dense)

    def one_well(low, vec):
        return jax.scipy.linalg.cho_solve((low, True), vec)

    solved = jax.vmap(one_well)(lower, rhs)
    return jnp.transpose(solved.reshape(count, segs, 3), (2, 0, 1))


def on_device(
    cell_state,
    cell_residual,
    cell_block,
    block_inverse,
    perf_cells,
    perf_count,
    perf_index,
    seg_parent,
    seg_cond,
    seg_state,
    seg_source,
):
    shard_cells = cell_state.shape[2]
    region_wells = perf_cells.shape[1]
    slots = perf_cells.shape[2]
    segs = seg_parent.shape[2]
    ncells = lax.axis_size("cells")
    me = lax.axis_index("cells")
    owned = region_wells // ncells
    first = me * owned
    state = cell_state[:, 0]
    resid = cell_residual[:, 0]
    start = me * shard_cells
    offset = perf_cells[0] - start
    inside = (offset >= 0) & (offset < shard_cells)
    safe = jnp.clip(offset, 0, shard_cells - 1)
    live = jnp.arange(slots, dtype=jnp.int32)[None, :] < perf_count[0][:, None]
    weight = jnp.where(inside & live, perf_index[0], jnp.float32(0.0))
    jac_at = cell_block[:, 0][:, safe]
    state_at = state[:, safe]
    kmat, flow = perf_terms(jac_at, state_at, weight, seg_state[:, 0])
    table = jnp.concatenate([kmat.reshape(9, region_wells, slots), flow], axis=0)
    table = segment_sums(table, segs)
    summed = lax.psum_scatter(table, "cells", scatter_dimension=1, tiled=True)
    parent = lax.dynamic_slice_in_dim(seg_parent[0], first, owned, 0)
    cond = lax.dynamic_slice_in_dim(seg_cond[0], first, owned, 0)
    source = lax.dynamic_slice_in_dim(seg_source[:, 0], first, owned, 1)
    wells_here = summed.shape[1]
    ksum = summed[:9].reshape(3, 3, wells_here, segs)
    rsum = summed[9:] + source
    solved = solve_wells(ksum, rsum, parent, cond)
    well_max = jnp.max(jnp.abs(rsum), axis=(1, 2))
    every_well = lax.all_gather(solved, "cells", axis=1, tiled=True)
    spread = expand_segments(every_well, slots)
    delta = jnp.sum(kmat * spread[None], axis=1)
    correction = (
        jnp.zeros((3, shard_cells), jnp.float32).at[:, safe.reshape(-1)].add(delta.reshape(3, -1))
    )
    corrected = resid - correction
    cell_max = jnp.max(jnp.abs(corrected), axis=1)
    cell_top, well_top = lax.pmax((cell_max, well_max), ("cells", "wells"))
    scale = 1.0 / jnp.maximum(jnp.float32(1.0), cell_top)
    inverse = block_inverse[:, 0].reshape(3, 3, shard_cells)
    step = jnp.sum(inverse * corrected[None], axis=1) * scale[:, None]
    residual_max = jnp.concatenate([cell_top, well_top])
    return (step[:, None], solved[:, None], residual_max)


def solution(mesh):
    in_specs = (
        P(None, "wells", "cells"),
        P(None, "wells", "cells"),
        P(None, "wells", "cells"),
        P(None, "wells", "cells"),
        P("wells", None, None),
        P("wells", None),
        P("wells", None, None),
        P("wells", None, None),
        P("wells", None, None),
        P(None, "wells", None, None),
        P(None, "wells", None, None),
    )
    out_specs = (P(None, "wells", "cells"), P(None, "wells", "cells", None), P())
    return jax.shard_map(
        on_device, mesh=mesh, in_specs=in_specs, out_specs=out_specs, check_vma=False
    )
```

profile of v0, /device:TPU:0, one launch (start us, length us, event | category | flops | bytes accessed | tf_op | source)
XLA Modules:
  0.0 272.6 jit_solution(10672945761370054616)
XLA Ops:
  0.7 0.8 fusion.23
  1.5 6.1 %copy.131 = f32[9,1,16384]{0,2,1:T(8,128)} copy(f32[9,1,16384]{2,1,0:T(1,128)} %param.13) | data formatting | bytes 1179648 | tf_op args[2]
  7.5 14.2 %gather_fusion = f32[4096,9]{1,0:T(8,128)S(1)} fusion(f32[9,16384]{0,1:T(8,128)} %bitcast.90, s32[4096]{0:T(1024)S(1)} %get-tuple-element.27), kind=kCustom, calls=%fused_computation | custom fusion | bytes 311296 | tf_op jit(solution)/shard_map/gather | solution.py:82
  22.5 4.6 %copy.138 = f32[3,1,16384]{0,2,1:T(8,128)} copy(f32[3,1,16384]{2,1,0:T(1,128)S(1)} %copy-done.3) | data formatting | bytes 393216 | tf_op args[0]
  27.1 17.5 %gather_fusion.1 = f32[4096,3]{1,0:T(8,128)} fusion(f32[3,16384]{0,1:T(8,128)} %bitcast.91, s32[4096]{0:T(1024)S(1)} %get-tuple-element.27), kind=kCustom, calls=%fused_computation.1 | custom fusion | bytes 114688 | tf_op jit(solution)/shard_map/gather | solution.py:83
  45.2 1.9 sub.50
  49.6 27.8 %all-reduce = f32[12,32,32]{2,1,0:T(8,128)S(1)} all-reduce(f32[12,32,32]{2,1,0:T(8,128)S(1)} %copy.142), channel_id=2, replica_groups=mesh['cells'=8,'wells'=4] {'cells'}, use_global_device_ids=true, to_apply=%region_4.5.clone | all-reduce | flops 12288 | bytes 98304
  78.9 3.1 %mul.160 = f32[4,32,3,32,3]{4,3,2,1,0:T(8,128)} broadcast(f32[4,32,3,3]{3,2,1,0:T(4,128)S(1)} %copy.143), dimensions={0,1,2,4} | broadcast | bytes 152064 | tf_op jit(solution)/shard_map/mul | solution.py:40
  81.9 6.5 %mul.161 = f32[4,96,96]{2,1,0:T(8,128)S(1)} reshape(f32[4,32,3,32,3]{4,3,2,1,0:T(8,128)} %mul.160) | data formatting | bytes 294912 | tf_op jit(solution)/shard_map/mul | solution.py:40
  89.9 3.5 %mul.150 = f32[4,32,3,32,3]{4,3,2,1,0:T(8,128)} broadcast(f32[4,32,32]{2,1,0:T(8,128)S(1)} %fusion.5), dimensions={0,1,3} | broadcast | bytes 163840 | tf_op jit(solution)/shard_map/mul | solution.py:39
  93.5 6.5 %mul.151 = f32[4,96,96]{2,1,0:T(8,128)S(1)} reshape(f32[4,32,3,32,3]{4,3,2,1,0:T(8,128)} %mul.150) | data formatting | bytes 294912 | tf_op jit(solution)/shard_map/mul | solution.py:39
  100.3 1.1 mul.153
  101.7 1.1 mul.163
  103.1 35.2 %custom-call.11 = f32[4,96,96]{2,1,0:T(8,128)S(1)} custom-call(f32[4,96,96]{2,1,0:T(8,128)S(1)} %fusion.9), custom_call_target="Cholesky" | custom-call | tf_op jit(solution)/shard_map/jit(cholesky)/cholesky | solution.py:44
  138.6 29.7 %custom-call.12 = f32[4,1,96,96]{2,3,1,0:T(8,128)S(1)} custom-call(f32[4,1,96,96]{3,2,1,0:T(8,128)S(1)} %select_bitcast_fusion), custom_call_target="InvertDiagBlocksLowerTriangular" | custom-call | tf_op jit(solution)/shard_map/vmap(jit(_cho_solve))/triangular_solve | solution.py:47
  168.3 0.8 abs_reduce_fusion.1
  170.3 8.4 %all_gather.3 = f32[3,32,32]{2,0,1:T(4,128)S(1)} all-gather(f32[3,4,32]{2,0,1:T(4,128)S(1)} %copy.148), channel_id=1, replica_groups=mesh['cells'=8,'wells'=4] {'cells'}, dimensions={1}, use_global_device_ids=true | all-gather | bytes 13824 | tf_op jit(solution)/shard_map/all_gather | solution.py:96
  179.8 29.1 %scatter_custom_fusion = f32[3,16384]{0,1:T(8,128)} fusion(s32[4096]{0:T(1024)S(1)} %bitcast.108, f32[4096,3]{1,0:T(8,128)S(1)} %copy.153, f32[]{:T(128)} %constant.69.clone.1), kind=kCustom, calls=%fused_computation.6 | custom fusion | flops 12288 | bytes 196612 | tf_op jit(solution)/shard_map/scatter-add | solution.py:100
  208.9 4.6 %copy.130 = f32[3,1,16384]{0,2,1:T(8,128)} copy(f32[3,1,16384]{2,1,0:T(1,128)S(1)} %copy-done.4) | data formatting | bytes 393216 | tf_op args[1]
  213.5 9.7 %abs_reduce_fusion = (f32[3]{0:T(128)S(1)}, f32[3,16384]{0,1:T(8,128)}) fusion(f32[3,16384]{0,1:T(8,128)} %scatter_custom_fusion, f32[3,1,16384]{0,2,1:T(8,128)} %copy.130), kind=kLoop, calls=%fused_computation.5 | loop fusion | flops 147453 | bytes 589836 | tf_op jit(solution)/shard_map/reduce_max | solution.py:103
  223.2 39.5 %all-reduce.1 = (f32[3]{0:T(128)S(1)}, f32[3]{0:T(128)S(1)}) all-reduce(f32[3]{0:T(128)S(1)} %get-tuple-element.23, f32[3]{0:T(128)S(1)} %get-tuple-element.29), channel_id=1, replica_groups=mesh['cells'=8,'wells'=4] {'cells','wells'}, use_global_device_ids=true, to_apply=%region_11.12 | all-reduce | flops 6 | bytes 48 | tf_op jit(solution)/shard_map/pmax | solution.py:104
  263.3 5.4 %copy.154 = f32[3,16384]{1,0:T(4,128)S(1)} copy(f32[3,16384]{0,1:T(8,128)} %get-tuple-element.24) | data formatting | bytes 393216 | tf_op jit(solution)/shard_map/sub | solution.py:102
  268.7 1.4 reduce.6
  271.0 0.9 reshape_multiply_fusion
  (78 shorter events, 11.4 us)
Async XLA Ops:
  0.6 87.9 %copy-start = (f32[1,32,32]{2,1,0:T(8,128)S(1)}, f32[1,32,32]{2,1,0:T(8,128)}, u32[]{:S(2)}) copy-start(f32[1,32,32]{2,1,0:T(8,128)} %param.19) | copy-start | bytes 12292
  0.6 21.7 %copy-start.5 = (s32[1,32,128]{2,1,0:T(8,128)S(1)}, s32[1,32,128]{2,1,0:T(8,128)}, u32[]{:S(2)}) copy-start(s32[1,32,128]{2,1,0:T(8,128)} %param.15) | copy-start | bytes 49156
  0.7 21.7 %copy-start.8 = (s32[1,32]{1,0:T(1,128)S(1)}, s32[1,32]{1,0:T(1,128)}, u32[]{:S(2)}) copy-start(s32[1,32]{1,0:T(1,128)} %param.16) | copy-start | bytes 388
  0.7 21.7 %copy-start.6 = (f32[1,32,128]{2,1,0:T(8,128)S(1)}, f32[1,32,128]{2,1,0:T(8,128)}, u32[]{:S(2)}) copy-start(f32[1,32,128]{2,1,0:T(8,128)} %param.17) | copy-start | bytes 49156
  0.7 21.8 %copy-start.3 = (f32[3,1,16384]{2,1,0:T(1,128)S(1)}, f32[3,1,16384]{2,1,0:T(1,128)}, u32[]{:S(2)}) copy-start(f32[3,1,16384]{2,1,0:T(1,128)} %param.11) | copy-start | bytes 589828
  7.5 37.1 %copy-start.7 = (f32[3,1,32,32]{3,2,1,0:T(8,128)S(1)}, f32[3,1,32,32]{3,2,1,0:T(8,128)}, u32[]{:S(2)}) copy-start(f32[3,1,32,32]{3,2,1,0:T(8,128)} %param.20) | copy-start | bytes 36868
  27.1 50.3 %copy-start.9 = (u32[32]{0:T(128)S(1)}, u32[32]{0:T(128)}, u32[]{:S(2)}) copy-start(u32[32]{0:T(128)} %constant.96) | copy-start | bytes 388
  101.7 107.1 %copy-start.4 = (f32[3,1,16384]{2,1,0:T(1,128)S(1)}, f32[3,1,16384]{2,1,0:T(1,128)}, u32[]{:S(2)}) copy-start(f32[3,1,16384]{2,1,0:T(1,128)} %param.12) | copy-start | bytes 589828
  213.5 59.1 %copy-start.1 = (f32[1,32,32]{2,1,0:T(8,128)S(1)}, f32[1,32,32]{2,1,0:T(8,128)}, u32[]{:S(2)}) copy-start(f32[1,32,32]{2,1,0:T(8,128)} %param.19) | copy-start | bytes 12292
  223.2 45.5 %copy-start.2 = (f32[9,1,16384]{2,1,0:T(1,128)S(1)}, f32[9,1,16384]{2,1,0:T(1,128)}, u32[]{:S(2)}) copy-start(f32[9,1,16384]{2,1,0:T(1,128)} %param.14) | copy-start | bytes 1769476
where the time goes:
time: 273 us
  other arithmetic  113 us (41%)
  local copies, waits for them, and re-layouts  81.6 us (30%)
  blocking collectives  75.7 us (28%)
    pmax x1, blocking collectives, on_device(): cell_top, well_top = lax.pmax((cell_max, well_max), ('cells', 'wells'))  39.5 us
    another operation x4, other arithmetic, solve_wells(): lower = jnp.linalg.cholesky(dense)  35.4 us
    another operation x3, other arithmetic, one_well(): return jax.scipy.linalg.cho_solve((low, True), vec)  29.8 us
    scatter-add x1, other arithmetic, on_device(): jnp.zeros((3, shard_cells), jnp.float32).at[:, safe.reshape(-1)]  29.1 us
    unnamed x1, blocking collectives  27.8 us
    gather x1, local copies, waits for them, and re-layouts, on_device(): state_at = state[:, safe]  17.5 us
    unnamed x27, local copies, waits for them, and re-layouts  16.8 us
    gather x2, local copies, waits for them, and re-layouts, on_device(): jac_at = cell_block[:, 0][:, safe]  14.8 us

commit v1 on v0

--- a/solution.py
+++ b/solution.py
@@ -93,7 +93,9 @@
     rsum = summed[9:] + source
     solved = solve_wells(ksum, rsum, parent, cond)
     well_max = jnp.max(jnp.abs(rsum), axis=(1, 2))
-    every_well = lax.all_gather(solved, "cells", axis=1, tiled=True)
+    every_well = jnp.concatenate(
+        lax.all_to_all(jnp.stack([solved] * lax.axis_size("cells")), "cells", 0, 0), axis=1
+    )
     spread = expand_segments(every_well, slots)
     delta = jnp.sum(kmat * spread[None], axis=1)
     correction = (

time: 273 us -> 271 us (level)
  blocking collectives: 75.7 us -> 67.3 us
  starting transfers between devices: 0 us -> 3.34 us
    all_gather x1 -> x0, blocking collectives: 8.42 us -> none  [on_device(): every_well = lax.all_gather(solved, 'cells', axis=1, tiled=True)]
    all_to_all x0 -> x1, starting transfers between devices: none -> 3.34 us  [on_device(): lax.all_to_all(jnp.stack([solved] * lax.axis_size('cells')), 'cells', 0, 0)]
    unnamed x27 -> x29, local copies, waits for them, and re-layouts: 16.8 us -> 17.6 us
  transfers between devices with their start and end apart: 0 -> 1, of which waited for: 0 -> 0; matrix products, arithmetic and copies ran while one was open for 0% -> 3% of each run, Pallas kernels for 0% -> 0%
where the time goes in v1:
time: 271 us; the launch traced here: 270 us
  other arithmetic  113 us (42%)
  local copies, waits for them, and re-layouts  84.3 us (31%)
  blocking collectives  67.3 us (25%)
  starting transfers between devices  3.34 us (1%)
    pmax x1, blocking collectives, on_device(): cell_top, well_top = lax.pmax((cell_max, well_max), ('cells', 'wells'))  39.5 us
    another operation x4, other arithmetic, solve_wells(): lower = jnp.linalg.cholesky(dense)  35.4 us
    another operation x3, other arithmetic, one_well(): return jax.scipy.linalg.cho_solve((low, True), vec)  29.8 us
    scatter-add x1, other arithmetic, on_device(): jnp.zeros((3, shard_cells), jnp.float32).at[:, safe.reshape(-1)]  29.4 us
    unnamed x1, blocking collectives  27.8 us
    unnamed x29, local copies, waits for them, and re-layouts  17.6 us
    gather x1, local copies, waits for them, and re-layouts, on_device(): state_at = state[:, safe]  17.5 us
    gather x2, local copies, waits for them, and re-layouts, on_device(): jac_at = cell_block[:, 0][:, safe]  14.8 us
  transfers between devices with their start and end apart: 1, of which 0 were waited for; matrix products, arithmetic and copies ran while one was open for 3% of the time, Pallas kernels for 0%

profile of v1, /device:TPU:0, one launch (start us, length us, event | category | flops | bytes accessed | tf_op | source)
XLA Modules:
  0.0 270.5 jit_solution(7044542929450102655)
XLA Ops:
  0.8 6.1 %copy.135 = f32[9,1,16384]{0,2,1:T(8,128)} copy(f32[9,1,16384]{2,1,0:T(1,128)} %param.13) | data formatting | bytes 1179648 | tf_op args[2]
  6.9 14.2 %gather_fusion = f32[4096,9]{1,0:T(8,128)S(1)} fusion(f32[9,16384]{0,1:T(8,128)} %bitcast.92, s32[4096]{0:T(1024)S(1)} %get-tuple-element.27), kind=kCustom, calls=%fused_computation | custom fusion | bytes 311296 | tf_op jit(solution)/shard_map/gather | solution.py:82
  21.9 4.6 %copy.142 = f32[3,1,16384]{0,2,1:T(8,128)} copy(f32[3,1,16384]{2,1,0:T(1,128)S(1)} %copy-done.3) | data formatting | bytes 393216 | tf_op args[0]
  26.5 17.5 %gather_fusion.1 = f32[4096,3]{1,0:T(8,128)} fusion(f32[3,16384]{0,1:T(8,128)} %bitcast.93, s32[4096]{0:T(1024)S(1)} %get-tuple-element.27), kind=kCustom, calls=%fused_computation.1 | custom fusion | bytes 114688 | tf_op jit(solution)/shard_map/gather | solution.py:83
  44.7 1.9 sub.50
  48.9 27.8 %all-reduce = f32[12,32,32]{2,1,0:T(8,128)S(1)} all-reduce(f32[12,32,32]{2,1,0:T(8,128)S(1)} %copy.146), channel_id=2, replica_groups=mesh['cells'=8,'wells'=4] {'cells'}, use_global_device_ids=true, to_apply=%region_4.5.clone | all-reduce | flops 12288 | bytes 98304
  78.2 3.1 %mul.160 = f32[4,32,3,32,3]{4,3,2,1,0:T(8,128)} broadcast(f32[4,32,3,3]{3,2,1,0:T(4,128)S(1)} %copy.147), dimensions={0,1,2,4} | broadcast | bytes 152064 | tf_op jit(solution)/shard_map/mul | solution.py:40
  81.2 6.5 %mul.161 = f32[4,96,96]{2,1,0:T(8,128)S(1)} reshape(f32[4,32,3,32,3]{4,3,2,1,0:T(8,128)} %mul.160) | data formatting | bytes 294912 | tf_op jit(solution)/shard_map/mul | solution.py:40
  89.2 3.5 %mul.150 = f32[4,32,3,32,3]{4,3,2,1,0:T(8,128)} broadcast(f32[4,32,32]{2,1,0:T(8,128)S(1)} %fusion.5), dimensions={0,1,3} | broadcast | bytes 163840 | tf_op jit(solution)/shard_map/mul | solution.py:39
  92.8 6.5 %mul.151 = f32[4,96,96]{2,1,0:T(8,128)S(1)} reshape(f32[4,32,3,32,3]{4,3,2,1,0:T(8,128)} %mul.150) | data formatting | bytes 294912 | tf_op jit(solution)/shard_map/mul | solution.py:39
  99.6 1.1 mul.153
  101.1 1.1 mul.163
  102.4 35.2 %custom-call.11 = f32[4,96,96]{2,1,0:T(8,128)S(1)} custom-call(f32[4,96,96]{2,1,0:T(8,128)S(1)} %fusion.9), custom_call_target="Cholesky" | custom-call | tf_op jit(solution)/shard_map/jit(cholesky)/cholesky | solution.py:44
  137.9 29.7 %custom-call.12 = f32[4,1,96,96]{2,3,1,0:T(8,128)S(1)} custom-call(f32[4,1,96,96]{3,2,1,0:T(8,128)S(1)} %select_bitcast_fusion), custom_call_target="InvertDiagBlocksLowerTriangular" | custom-call | tf_op jit(solution)/shard_map/vmap(jit(_cho_solve))/triangular_solve | solution.py:47
  167.6 0.8 abs_reduce_fusion.1
  170.3 3.3 %all-to-all-start = ((f32[8,1,384]{2,1,0:T(1,128)}), f32[8,1,384]{2,1,0:T(1,128)S(1)}, u32[]{:S(2)}, u32[]{:S(2)}) async-start(f32[8,1,384]{2,1,0:T(1,128)} %reshape.325), calls=%async_computation | async-start | bytes 24576 | tf_op jit(solution)/shard_map/all_to_all | solution.py:97
  173.7 4.6 %copy.134 = f32[3,1,16384]{0,2,1:T(8,128)} copy(f32[3,1,16384]{2,1,0:T(1,128)S(1)} %copy-done.4) | data formatting | bytes 393216 | tf_op args[1]
  178.3 1.4 reduce.6
  182.4 2.0 copy.158
  184.4 29.4 %scatter_custom_fusion = f32[3,16384]{0,1:T(8,128)} fusion(s32[4096]{0:T(1024)S(1)} %bitcast.112, f32[4096,3]{1,0:T(8,128)} %copy.158, f32[]{:T(128)} %constant.69.clone.1), kind=kCustom, calls=%fused_computation.6 | custom fusion | flops 12288 | bytes 197120 | tf_op jit(solution)/shard_map/scatter-add | solution.py:102
  213.8 9.7 %abs_reduce_fusion = (f32[3]{0:T(128)S(1)}, f32[3,16384]{0,1:T(8,128)}) fusion(f32[3,16384]{0,1:T(8,128)} %scatter_custom_fusion, f32[3,1,16384]{0,2,1:T(8,128)} %copy.134), kind=kLoop, calls=%fused_computation.5 | loop fusion | flops 147453 | bytes 589836 | tf_op jit(solution)/shard_map/reduce_max | solution.py:105
  223.5 39.5 %all-reduce.1 = (f32[3]{0:T(128)S(1)}, f32[3]{0:T(128)S(1)}) all-reduce(f32[3]{0:T(128)S(1)} %get-tuple-element.23, f32[3]{0:T(128)S(1)} %get-tuple-element.29), channel_id=1, replica_groups=mesh['cells'=8,'wells'=4] {'cells','wells'}, use_global_device_ids=true, to_apply=%region_11.12 | all-reduce | flops 6 | bytes 48 | tf_op jit(solution)/shard_map/pmax | solution.py:106
  263.6 5.4 %copy.159 = f32[3,16384]{1,0:T(4,128)S(1)} copy(f32[3,16384]{0,1:T(8,128)} %get-tuple-element.24) | data formatting | bytes 393216 | tf_op jit(solution)/shard_map/sub | solution.py:104
  269.6 0.9 reshape_multiply_fusion
  (85 shorter events, 12.8 us)
Async XLA Ops:
  0.6 87.2 %copy-start = (f32[1,32,32]{2,1,0:T(8,128)S(1)}, f32[1,32,32]{2,1,0:T(8,128)}, u32[]{:S(2)}) copy-start(f32[1,32,32]{2,1,0:T(8,128)} %param.19) | copy-start | bytes 12292
  0.6 6.2 %copy-start.5 = (s32[1,32,128]{2,1,0:T(8,128)S(1)}, s32[1,32,128]{2,1,0:T(8,128)}, u32[]{:S(2)}) copy-start(s32[1,32,128]{2,1,0:T(8,128)} %param.15) | copy-start | bytes 49156
  0.7 21.0 %copy-start.6 = (f32[1,32,128]{2,1,0:T(8,128)S(1)}, f32[1,32,128]{2,1,0:T(8,128)}, u32[]{:S(2)}) copy-start(f32[1,32,128]{2,1,0:T(8,128)} %param.17) | copy-start | bytes 49156
  0.7 21.1 %copy-start.8 = (s32[1,32]{1,0:T(1,128)S(1)}, s32[1,32]{1,0:T(1,128)}, u32[]{:S(2)}) copy-start(s32[1,32]{1,0:T(1,128)} %param.16) | copy-start | bytes 388
  0.7 21.2 %copy-start.3 = (f32[3,1,16384]{2,1,0:T(1,128)S(1)}, f32[3,1,16384]{2,1,0:T(1,128)}, u32[]{:S(2)}) copy-start(f32[3,1,16384]{2,1,0:T(1,128)} %param.11) | copy-start | bytes 589828
  6.8 37.2 %copy-start.7 = (f32[3,1,32,32]{3,2,1,0:T(8,128)S(1)}, f32[3,1,32,32]{3,2,1,0:T(8,128)}, u32[]{:S(2)}) copy-start(f32[3,1,32,32]{3,2,1,0:T(8,128)} %param.20) | copy-start | bytes 36868
  26.5 50.2 %copy-start.9 = (u32[32]{0:T(128)S(1)}, u32[32]{0:T(128)}, u32[]{:S(2)}) copy-start(u32[32]{0:T(128)} %constant.96) | copy-start | bytes 388
  92.8 80.9 %copy-start.4 = (f32[3,1,16384]{2,1,0:T(1,128)S(1)}, f32[3,1,16384]{2,1,0:T(1,128)}, u32[]{:S(2)}) copy-start(f32[3,1,16384]{2,1,0:T(1,128)} %param.12) | copy-start | bytes 589828
  99.6 78.7 %copy-start.2 = (f32[9,1,16384]{2,1,0:T(1,128)S(1)}, f32[9,1,16384]{2,1,0:T(1,128)}, u32[]{:S(2)}) copy-start(f32[9,1,16384]{2,1,0:T(1,128)} %param.14) | copy-start | bytes 1769476
  170.3 10.4 %all-to-all-start = ((f32[8,1,384]{2,1,0:T(1,128)}), f32[8,1,384]{2,1,0:T(1,128)S(1)}, u32[]{:S(2)}, u32[]{:S(2)}) async-start(f32[8,1,384]{2,1,0:T(1,128)} %reshape.325), calls=%async_computation | async-start | bytes 24576 | tf_op jit(solution)/shard_map/all_to_all | solution.py:97
  213.8 56.7 %copy-start.1 = (f32[1,32,32]{2,1,0:T(8,128)S(1)}, f32[1,32,32]{2,1,0:T(8,128)}, u32[]{:S(2)}) copy-start(f32[1,32,32]{2,1,0:T(8,128)} %param.19) | copy-start | bytes 12292
